TPU v7x, 32 devices: a whole 2x2x4 slice. The times are simulated.
32 devices in a mesh: tm: 4 (over y, core), rows: 8 (over z, x).
Axes of the slice: x: 2, y: 2, z: 4, core: 2. Of those that a mesh axis runs over, the one named last changes fastest.
Arguments:
- features: bfloat16 [4, 24, 64, 512], P('tm', 'rows'), may hold values from -64 to 64, as said below
- gamma: float32 [512], replicated, may hold values from 0.1 to 1.9
- beta: float32 [512], replicated, may hold values from -3 to 3
- kernel: bfloat16 [3, 512, 3, 3, 512], P(None, 'tm'), may hold values from -0.0546875 to 0.0546875
- bias: float32 [512], replicated, may hold values from -3 to 3
Outputs:
- decoded: bfloat16 [4, 24, 64, 512], P('tm', 'rows')
Inputs may be any that keep to these rules, and one draw needn't show every extreme that they name: features are finite.
All inputs are finite; a program needn't handle non-finite values.
Results may differ from a plain program's by a relative error of at most 0.004.
Values may be sent and summed in bfloat16 or wider, within the bound.
A program may use at most 128 MiB of HBM per device.

v0:
```python
import jax
import jax.numpy as jnp
from jax import lax
from jax.sharding import PartitionSpec as P

GROUPS = 32


EPSILON = 1e-06


def shifted(x, axis, by):
    length = lax.axis_size(axis)
    pairs = [(i, i + by) for i in range(length) if 0 <= i + by < length]
    return lax.ppermute(x, axis, pairs)


def extended_2(x, sides, width):
    for axis, dim in sides:
        size, length = (lax.axis_size(axis), x.shape[dim])
        up = [(i, (i + 1) % size) for i in range(size - 1)]
        down = [(j, i) for i, j in up]
        last = lax.slice_in_dim(x, length - width, length, axis=dim)
        first = lax.slice_in_dim(x, 0, width, axis=dim)
        before = lax.ppermute(last, axis, up)
        after = lax.ppermute(first, axis, down)
        x = jnp.concatenate([before, x, after], axis=dim)
    return x


def unfold(block, height, across):
    pieces = []
    for tap_row in range(3):
        for tap_col in range(3):
            pieces.append(block[:, tap_row : tap_row + height, tap_col : tap_col + across, :])
    return jnp.concatenate(pieces, axis=-1)


def flatten_taps(taps):
    return taps.reshape(3, taps.shape[1], -1)


def apply_taps(columns, taps, frames):
    flat = flatten_taps(taps)
    total = jnp.einsum(
        "fhwc,kc->fhwk", columns[0:frames], flat[0], preferred_element_type=jnp.float32
    )
    for tap_time in (1, 2):
        total = total + jnp.einsum(
            "fhwc,kc->fhwk",
            columns[tap_time : tap_time + frames],
            flat[tap_time],
            preferred_element_type=jnp.float32,
        )
    return total


def widen(block):
    return jnp.pad(block, ((0, 0), (0, 0), (1, 1), (0, 0)))


def previous_span(block):
    return shifted(block, "tm", 1)


def local(features, gamma, beta, kernel, bias):
    frames, height, across, channels = features.shape
    values = features.astype(jnp.float32)
    grouped = values.reshape(frames, height, across, GROUPS, channels // GROUPS)
    count = float(
        frames
        * height
        * across
        * (channels // GROUPS)
        * lax.axis_size("tm")
        * lax.axis_size("rows")
    )
    totals, squares = lax.psum(
        (jnp.sum(grouped, axis=(0, 1, 2, 4)), jnp.sum(grouped * grouped, axis=(0, 1, 2, 4))),
        ("tm", "rows"),
    )
    center = totals / count
    spread = squares / count - center * center
    centered = grouped - center[:, None]
    normed = (centered * lax.rsqrt(spread + EPSILON)[:, None]).reshape(
        frames, height, across, channels
    )
    active = jax.nn.silu(normed * gamma + beta).astype(jnp.bfloat16)
    rimmed = extended_2(active, (("rows", 1),), 1)
    first_span = lax.axis_index("tm") == 0
    minus_one = jnp.where(first_span, rimmed, previous_span(rimmed))
    minus_two = jnp.where(first_span, rimmed, previous_span(minus_one))
    cache = jnp.concatenate([minus_two, minus_one], axis=0)
    extended = widen(jnp.concatenate([cache, rimmed], axis=0))
    columns = unfold(extended, height, across)
    conv = apply_taps(columns, lax.all_gather(kernel, "tm", axis=1, tiled=True), frames)
    return (values + conv + bias).astype(jnp.bfloat16)


def solution(mesh):
    in_specs = (P("tm", "rows", None, None), P(), P(), P(None, "tm", None, None, None), P())
    out_specs = P("tm", "rows", None, None)
    return jax.shard_map(local, mesh=mesh, in_specs=in_specs, out_specs=out_specs, check_vma=False)
```

profile of v0, /device:TPU:13, one launch (start us, length us, event | category | flops | bytes accessed | tf_op | source)
XLA Modules:
  0.0 135.2 jit_solution(9544178804054469499)
XLA Ops:
  6.5 6.1 %copy.9 = bf16[3,128,3,3,512]{1,4,3,2,0:T(8,128)(2,1)} copy(bf16[3,128,3,3,512]{4,1,3,2,0:T(8,128)(2,1)} %param.8) | data formatting | bytes 7077888 | tf_op args[3]
  12.7 0.1 reduce_sum.36
  12.8 0.1 reduce_sum.24
  12.9 0.1 reduce_sum.37
  13.0 0.1 reduce_sum.25
  13.1 40.4 %all-reduce.1 = (f32[32]{0:T(128)S(1)}, f32[32]{0:T(128)S(1)}) all-reduce(f32[32]{0:T(128)S(1)} %reduce_sum.37, f32[32]{0:T(128)S(1)} %reduce_sum.25), channel_id=1, replica_groups=mesh['tm'=4,'rows'=8] {'tm','rows'}, use_global_device_ids=true, to_apply=%region_5.6 | all-reduce | flops 64 | bytes 512 | tf_op jit(solution)/shard_map/psum | solution.py:78
  53.6 0.1 mul.44
  53.7 0.1 sub.20
  53.8 0.1 fusion.23
  54.0 3.0 %collective-permute-start.1 = (bf16[1,1,64,512]{3,2,1,0:T(8,128)(2,1)S(1)}, bf16[1,1,64,512]{3,2,1,0:T(8,128)(2,1)S(1)}, u32[]{:S(2)}, u32[]{:S(2)}) collective-permute-start(bf16[1,1,64,512]{3,2,1,0:T(8,128)(2,1)S(1)} %get-tuple-element.13), channel_id=1, source_target_pairs={{1,0},{2,1},{3,2},{4,3},{5,4},{6,5},{7,6},{9,8},{10,9},{11,10},{12... | collective-permute-start | bytes 196616 | tf_op jit(solution)/shard_map/ppermute | solution.py:26
  57.0 2.3 %collective-permute-start = (bf16[1,1,64,512]{3,2,1,0:T(8,128)(2,1)S(1)}, bf16[1,1,64,512]{3,2,1,0:T(8,128)(2,1)S(1)}, u32[]{:S(2)}, u32[]{:S(2)}) collective-permute-start(bf16[1,1,64,512]{3,2,1,0:T(8,128)(2,1)S(1)} %get-tuple-element.12), channel_id=1, source_target_pairs={{0,1},{1,2},{2,3},{3,4},{4,5},{5,6},{6,7},{8,9},{9,10},{10,11},{11... | collective-permute-start | bytes 196616 | tf_op jit(solution)/shard_map/ppermute | solution.py:25
  59.3 0.1 collective-permute-done.1
  59.4 3.5 %collective-permute-done = bf16[1,1,64,512]{3,2,1,0:T(8,128)(2,1)S(1)} collective-permute-done((bf16[1,1,64,512]{3,2,1,0:T(8,128)(2,1)S(1)}, bf16[1,1,64,512]{3,2,1,0:T(8,128)(2,1)S(1)}, u32[]{:S(2)}, u32[]{:S(2)}) %collective-permute-start) | collective-permute-done | bytes 65568 | tf_op jit(solution)/shard_map/ppermute | solution.py:25
  63.0 1.3 collective-permute-start.2
  64.3 5.3 %collective-permute-done.2 = bf16[1,5,64,512]{3,2,1,0:T(8,128)(2,1)S(1)} collective-permute-done((bf16[1,5,64,512]{3,2,1,0:T(8,128)(2,1)S(1)}, bf16[1,5,64,512]{3,2,1,0:T(8,128)(2,1)S(1)}, u32[]{:S(2)}, u32[]{:S(2)}) %collective-permute-start.2) | collective-permute-done | bytes 327712 | tf_op jit(solution)/shard_map/ppermute | solution.py:15
  69.7 1.3 collective-permute-start.3
  71.0 13.8 %collective-permute-done.3 = bf16[1,5,64,512]{3,2,1,0:T(8,128)(2,1)S(1)} collective-permute-done((bf16[1,5,64,512]{3,2,1,0:T(8,128)(2,1)S(1)}, bf16[1,5,64,512]{3,2,1,0:T(8,128)(2,1)S(1)}, u32[]{:S(2)}, u32[]{:S(2)}) %collective-permute-start.3) | collective-permute-done | bytes 327712 | tf_op jit(solution)/shard_map/ppermute | solution.py:15
  84.8 0.1 maximum_maximum_fusion
  84.9 1.0 fusion.9
  85.9 0.9 slice_dynamic-update-slice_fusion.2
  86.8 1.0 fusion.10
  87.8 1.0 fusion.11
  88.8 0.9 slice_dynamic-update-slice_fusion.1
  89.8 1.0 fusion.12
  90.8 1.0 fusion.13
  91.8 1.0 slice_dynamic-update-slice_fusion
  92.8 1.0 fusion.14
  93.8 20.4 %all-gather.2.cloned.1.call-done = bf16[3,512,3,3,512]{1,4,3,2,0:T(8,128)(2,1)} async-done(((bf16[3,128,3,3,512]{1,4,3,2,0:T(8,128)(2,1)}), bf16[3,512,3,3,512]{1,4,3,2,0:T(8,128)(2,1)}) %all-gather.2.cloned.1.call-update) | async-done | bytes 14155792 | tf_op jit(solution)/shard_map/all_gather | solution.py:96
  114.2 5.7 %fusion.25 = (bf16[1,512,3,3,512]{1,4,3,2,0:T(8,128)(2,1)S(1)}, bf16[1,512,3,3,512]{1,4,3,2,0:T(8,128)(2,1)S(1)}, bf16[1,512,3,3,512]{1,4,3,2,0:T(8,128)(2,1)S(1)}) fusion(bf16[3,512,3,3,512]{1,4,3,2,0:T(8,128)(2,1)} %all-gather.2.cloned.1.call-done), kind=kLoop, calls=%fused_computation.46 | loop fusion | bytes 28311552 | tf_op jit(solution)/shard_map/slice | solution.py:46
  120.0 2.5 %fusion = f32[3,64,512]{2,1,0:T(8,128)S(1)} fusion(bf16[512,4608,1]{0,1,2:T(8,128)(2,1)S(1)} %bitcast.43, bf16[3,3,64,4608]{3,2,1,0:T(8,128)(2,1)} %fusion.14), kind=kOutput, calls=%fused_computation.1 | convolution fusion | flops 905969664 | bytes 6881280 | tf_op jit(solution)/shard_map/fhwc,kc->fhwk/dot_general | solution.py:49
  122.5 2.6 %fusion.1 = f32[3,64,512]{2,1,0:T(8,128)S(1)} fusion(bf16[512,4608,1]{0,1,2:T(8,128)(2,1)S(1)} %bitcast.42, bf16[3,3,64,4608]{3,2,1,0:T(8,128)(2,1)} %fusion.14), kind=kOutput, calls=%fused_computation.3 | convolution fusion | flops 905969664 | bytes 6881280 | tf_op jit(solution)/shard_map/fhwc,kc->fhwk/dot_general | solution.py:49
  125.1 3.3 %fusion.8 = bf16[1,3,64,512]{3,2,1,0:T(8,128)(2,1)} fusion(f32[3,64,512]{2,1,0:T(8,128)S(1)} %fusion, f32[3,64,512]{2,1,0:T(8,128)S(1)} %fusion.1, bf16[512,4608,1]{0,1,2:T(8,128)(2,1)S(1)} %bitcast.41, bf16[3,3,64,4608]{3,2,1,0:T(8,128)(2,1)} %fusion.14, bf16[1,3,64,512]{3,2,1,0:T(8,128)(2,1)S(1)} %copy-done, f32[512]{0:T(512)S(1)} %copy-done.3), kind=kOutput, calls=%fused_computation.11 | convolution fusion | flops 906559488 | bytes 7669760 | tf_op jit(solution)/shard_map/fhwc,kc->fhwk/dot_general | solution.py:45
  (18 shorter events, 0.4 us)
Async XLA Ops:
  6.5 6.1 %copy-start = (bf16[1,3,64,512]{3,2,1,0:T(8,128)(2,1)S(1)}, bf16[1,3,64,512]{3,2,1,0:T(8,128)(2,1)}, u32[]{:S(2)}) copy-start(bf16[1,3,64,512]{3,2,1,0:T(8,128)(2,1)} %param.5) | copy-start | bytes 589828
  6.5 47.3 %copy-start.1 = (f32[512]{0:T(512)S(1)}, f32[512]{0:T(512)}, u32[]{:S(2)}) copy-start(f32[512]{0:T(512)} %param.7) | copy-start | bytes 6148
  6.5 47.3 %copy-start.2 = (f32[512]{0:T(512)S(1)}, f32[512]{0:T(512)}, u32[]{:S(2)}) copy-start(f32[512]{0:T(512)} %param.6) | copy-start | bytes 6148
  6.5 107.7 %all-gather.2.cloned.1.call-start = ((), (), s32[]{:S(2)}) async-start(), calls=%async_computation | async-start | bytes 17694720 | tf_op jit(solution)/shard_map/all_gather | solution.py:96
  54.0 5.4 %collective-permute-start.1 = (bf16[1,1,64,512]{3,2,1,0:T(8,128)(2,1)S(1)}, bf16[1,1,64,512]{3,2,1,0:T(8,128)(2,1)S(1)}, u32[]{:S(2)}, u32[]{:S(2)}) collective-permute-start(bf16[1,1,64,512]{3,2,1,0:T(8,128)(2,1)S(1)} %get-tuple-element.13), channel_id=1, source_target_pairs={{1,0},{2,1},{3,2},{4,3},{5,4},{6,5},{7,6},{9,8},{10,9},{11,10},{12... | collective-permute-start | bytes 196616 | tf_op jit(solution)/shard_map/ppermute | solution.py:26
  57.0 6.0 %collective-permute-start = (bf16[1,1,64,512]{3,2,1,0:T(8,128)(2,1)S(1)}, bf16[1,1,64,512]{3,2,1,0:T(8,128)(2,1)S(1)}, u32[]{:S(2)}, u32[]{:S(2)}) collective-permute-start(bf16[1,1,64,512]{3,2,1,0:T(8,128)(2,1)S(1)} %get-tuple-element.12), channel_id=1, source_target_pairs={{0,1},{1,2},{2,3},{3,4},{4,5},{5,6},{6,7},{8,9},{9,10},{10,11},{11... | collective-permute-start | bytes 196616 | tf_op jit(solution)/shard_map/ppermute | solution.py:25
  63.0 6.6 %collective-permute-start.2 = (bf16[1,5,64,512]{3,2,1,0:T(8,128)(2,1)S(1)}, bf16[1,5,64,512]{3,2,1,0:T(8,128)(2,1)S(1)}, u32[]{:S(2)}, u32[]{:S(2)}) collective-permute-start(bf16[1,5,64,512]{3,2,1,0:T(8,128)(2,1)S(1)} %pad_maximum_fusion), channel_id=1, source_target_pairs={{0,8},{8,16},{16,24},{1,9},{9,17},{17,25},{2,10},{10,18},{18,26},{... | collective-permute-start | bytes 983048 | tf_op jit(solution)/shard_map/ppermute | solution.py:15
  69.7 15.1 %collective-permute-start.3 = (bf16[1,5,64,512]{3,2,1,0:T(8,128)(2,1)S(1)}, bf16[1,5,64,512]{3,2,1,0:T(8,128)(2,1)S(1)}, u32[]{:S(2)}, u32[]{:S(2)}) collective-permute-start(bf16[1,5,64,512]{3,2,1,0:T(8,128)(2,1)S(1)} %broadcast_select_fusion.1), channel_id=1, source_target_pairs={{0,8},{8,16},{16,24},{1,9},{9,17},{17,25},{2,10},{10,18},{18,26},{... | collective-permute-start | bytes 983048 | tf_op jit(solution)/shard_map/ppermute | solution.py:15
  122.5 2.6 %copy-start.3 = (f32[512]{0:T(512)S(1)}, f32[512]{0:T(512)}, u32[]{:S(2)}) copy-start(f32[512]{0:T(512)} %param.9) | copy-start | bytes 6148
Sparse Core Ops, SparseCore 0:
  12.8 101.4 all-gather.1
where the time goes:
time: 136 us; the launch traced here: 135 us
  waiting for transfers between devices  43.1 us (32%)
  blocking collectives  40.4 us (30%)
  local copies, waits for them, and re-layouts  21.2 us (16%)
  between operations  13.5 us (10%)
  matrix products  8.36 us (6%)
  starting transfers between devices  7.87 us (6%)
    psum x1, blocking collectives, local(): lax.psum((jnp.sum(grouped, axis=(0, 1, 2, 4)), jnp.sum(grouped * grouped,...  40.4 us
    all_gather x1, waiting for transfers between devices, local(): lax.all_gather(kernel, 'tm', axis=1, tiled=True)  20.4 us
    ppermute x2, waiting for transfers between devices, shifted(): return lax.ppermute(x, axis, pairs)  19.1 us
    unnamed x17, local copies, waits for them, and re-layouts  14 us
    slice x1, local copies, waits for them, and re-layouts, apply_taps(): flat[0]  5.74 us
    dot_general x2, matrix products, apply_taps(): jnp.einsum('fhwc,kc->fhwk', columns[tap_time:tap_time + frames], flat[tap...  5.1 us
    ppermute x1, waiting for transfers between devices, extended_2(): before = lax.ppermute(last, axis, up)  3.54 us
    dot_general x1, matrix products, apply_taps(): jnp.einsum('fhwc,kc->fhwk', columns[0:frames], flat[0], preferred_element...  3.26 us
  transfers between devices with their start and end apart: 5, of which 5 were waited for; matrix products, arithmetic and copies ran while one was open for 7% of the time, Pallas kernels for 0%

commit v1 on v0

v1 whole, which is shorter than its diff:
```python
import functools

import jax
import jax.numpy as jnp
from jax import lax
from jax.experimental import pallas as pl
from jax.experimental.pallas import tpu as pltpu
from jax.sharding import PartitionSpec as P

GROUPS = 32
EPSILON = 1e-06
LANES = 128
MESH = pl.DeviceIdType.MESH
CORES = 2


def group_sum(x, span):
    lane = lax.broadcasted_iota(jnp.int32, x.shape, 1)
    step = 1
    while step < span:
        upper = pltpu.roll(x, LANES - step, 1)
        lower = pltpu.roll(x, step, 1)
        x = x + jnp.where((lane & step) == 0, upper, lower)
        step *= 2
    return x


def body(nt, nr, features, gamma, beta, weights, bias, out, raw, xs, wp, w0, prod, stats,
         block, feat_sem, w_sem, stat_send, stat_recv, halo_send, sib_send, peer_send,
         recv, out_send, out_recv):
    ny = nt // CORES
    total = nt * nr
    _, height, across, channels = features.shape
    outs = weights.shape[3]
    chunks = channels // LANES
    span = channels // GROUPS
    tm = lax.axis_index("tm")
    row = lax.axis_index("rows")
    y = tm // CORES
    core = lax.rem(tm, CORES)
    sib = y * CORES + (1 - core)
    me = tm * nr + row
    pieces = ((0, 1), (1, height), (height + 1, 1))

    def tap_copies():
        for b in range(3):
            for c in range(3):
                cols = pl.ds(c * channels, channels)
                yield pltpu.make_async_copy(weights.at[0, b, c], w0.at[b, :, cols], w_sem.at[0])
                for a in (1, 2):
                    yield pltpu.make_async_copy(
                        weights.at[a, b, c], wp.at[b, pl.ds((a - 1) * outs, outs), cols],
                        w_sem.at[1])

    own = pltpu.make_async_copy(features, raw.at[pl.ds(tm, 1), pl.ds(1, height)], feat_sem)
    own.start()
    barrier = pltpu.get_barrier_semaphore()

    def greet(i, carry):
        other = lax.rem(me + i, total)
        pl.semaphore_signal(barrier, inc=1, device_id=(other // nr, lax.rem(other, nr)),
                            device_id_type=MESH)
        return carry

    lax.fori_loop(1, total, greet, 0)
    for copy in tap_copies():
        copy.start()
    own.wait()

    values = raw[tm, 1:1 + height].astype(jnp.float32).reshape(height * across, channels)
    count = float(height * across * span)
    sums = jnp.sum(values, axis=0, keepdims=True)
    rows8 = jnp.concatenate([sums[:, i * LANES:(i + 1) * LANES] for i in range(chunks)], axis=0)
    means = group_sum(rows8, span) * (1.0 / count)
    wide = jnp.concatenate([means[i:i + 1] for i in range(chunks)], axis=1)
    centred = values - wide
    squares = jnp.sum(centred * centred, axis=0, keepdims=True)
    rows8 = jnp.concatenate([squares[:, i * LANES:(i + 1) * LANES] for i in range(chunks)], axis=0)
    moments = group_sum(rows8, span)
    place = lax.broadcasted_iota(jnp.int32, (1, LANES), 1) % span
    packed = jnp.zeros((1, LANES), jnp.float32)
    for i in range(chunks):
        packed = jnp.where(place == i, means[i:i + 1], packed)
        packed = jnp.where(place == chunks + i, moments[i:i + 1], packed)
    stats[me] = packed

    pl.semaphore_wait(barrier, total - 1)

    def stat_copy(i):
        other = lax.rem(me + i, total)
        return pltpu.make_async_remote_copy(
            src_ref=stats.at[me], dst_ref=stats.at[me], send_sem=stat_send, recv_sem=stat_recv,
            device_id=(other // nr, lax.rem(other, nr)), device_id_type=MESH)

    def send_stat(i, carry):
        stat_copy(i).start()
        return carry

    lax.fori_loop(1, total, send_stat, 0)

    def piece(f, p):
        first, size = pieces[p]
        return raw.at[f, pl.ds(first, size)]

    def to_sib(f, p):
        return pltpu.make_async_remote_copy(
            src_ref=piece(f, p), dst_ref=piece(f, p), send_sem=sib_send.at[f, p],
            recv_sem=recv.at[f, p], device_id=(sib, row), device_id_type=MESH)

    def to_peer(d, p):
        other = lax.rem(y + d, ny) * CORES + core
        return pltpu.make_async_remote_copy(
            src_ref=piece(tm, p), dst_ref=piece(tm, p), send_sem=peer_send.at[d, p],
            recv_sem=recv.at[tm, p], device_id=(other, row), device_id_type=MESH)

    def from_any(f, p):
        return pltpu.make_async_remote_copy(
            src_ref=piece(f, p), dst_ref=piece(f, p), send_sem=sib_send.at[f, p],
            recv_sem=recv.at[f, p], device_id=(sib, row), device_id_type=MESH)

    up_copy = pltpu.make_async_remote_copy(
        src_ref=raw.at[tm, pl.ds(height, 1)], dst_ref=raw.at[tm, pl.ds(0, 1)],
        send_sem=halo_send.at[0], recv_sem=recv.at[tm, 0],
        device_id=(tm, jnp.minimum(row + 1, nr - 1)), device_id_type=MESH)
    down_copy = pltpu.make_async_remote_copy(
        src_ref=raw.at[tm, pl.ds(1, 1)], dst_ref=raw.at[tm, pl.ds(height + 1, 1)],
        send_sem=halo_send.at[1], recv_sem=recv.at[tm, 2],
        device_id=(tm, jnp.maximum(row - 1, 0)), device_id_type=MESH)
    has_above = row > 0
    has_below = row < nr - 1

    @pl.when(has_below)
    def _():
        up_copy.start()

    @pl.when(has_above)
    def _():
        down_copy.start()

    def loop_peers(fn):
        def step(d, carry):
            fn(d)
            return carry
        lax.fori_loop(1, ny, step, 0)

    loop_peers(lambda d: to_peer(d, 1).start())
    to_sib(tm, 1).start()

    for p, there in ((0, has_above), (2, has_below)):
        @pl.when(there)
        def _(p=p):
            from_any(tm, p).wait_recv()
            loop_peers(lambda d: to_peer(d, p).start())
            to_sib(tm, p).start()

    pltpu.make_async_remote_copy(
        src_ref=stats.at[pl.ds(0, total - 1)], dst_ref=stats.at[pl.ds(0, total - 1)],
        send_sem=stat_send, recv_sem=stat_recv, device_id=(sib, row),
        device_id_type=MESH).wait()
    every = stats[...].reshape(total, LANES)
    summed = jnp.sum(every, axis=0, keepdims=True)
    middle = summed * (1.0 / total)
    away = every - middle
    away = jnp.sum(away * away, axis=0, keepdims=True) * count
    rows = []
    for i in range(chunks):
        rows.append(jnp.where(place == i, middle, 0.0))
    for i in range(chunks):
        rows.append(jnp.where(place == chunks + i, summed, 0.0)
                    + jnp.where(place == i, away, 0.0))
    spread_out = group_sum(jnp.concatenate(rows, axis=0), span)
    center = jnp.concatenate([spread_out[i:i + 1] for i in range(chunks)], axis=1)
    spread = jnp.concatenate(
        [spread_out[chunks + i:chunks + i + 1] for i in range(chunks)], axis=1)
    spread = spread * (1.0 / (count * total))
    gain = lax.rsqrt(spread + EPSILON) * gamma[...]
    shift = beta[...]

    column = lax.broadcasted_iota(jnp.int32, (across, channels), 0)

    def activate_row(f, i):
        v = (raw[f, i].astype(jnp.float32) - center) * gain + shift
        v = v * 0.5
        v = v * jnp.tanh(v) + v
        before = jnp.where(column == 0, 0.0, pltpu.roll(v, 1, 0))
        after = jnp.where(column == across - 1, 0.0, pltpu.roll(v, across - 1, 0))
        xs[f, i, :, 0:channels] = before.astype(jnp.bfloat16)
        xs[f, i, :, channels:2 * channels] = v.astype(jnp.bfloat16)
        xs[f, i, :, 2 * channels:] = after.astype(jnp.bfloat16)

    def edge_row(f, i, there):
        @pl.when(there)
        def _():
            activate_row(f, i)

        @pl.when(jnp.logical_not(there))
        def _():
            xs[f, i] = jnp.zeros((across, 3 * channels), jnp.bfloat16)

    def dot(f, taps, b):
        left = xs[f, b:b + height].reshape(height * across, 3 * channels)
        return lax.dot_general(left, taps[b], (((1,), (1,)), ((), ())),
                               preferred_element_type=jnp.float32)

    def process(f):
        for i in range(1, height + 1):
            activate_row(f, i)
        edge_row(f, 0, has_above)
        edge_row(f, height + 1, has_below)
        pair = dot(f, wp, 0) + dot(f, wp, 1) + dot(f, wp, 2)
        prod[f, 1] = pair[:, 0:outs]
        prod[f, 2] = pair[:, outs:2 * outs]

        @pl.when(jnp.logical_or(f == 0, f + 2 < nt))
        def _():
            prod[f, 0] = dot(f, w0, 0) + dot(f, w0, 1) + dot(f, w0, 2)

    def wait_frame(f, forward):
        from_any(f, 1).wait_recv()
        if forward:
            to_sib(f, 1).start()
        for p, there in ((0, has_above), (2, has_below)):
            @pl.when(there)
            def _(p=p):
                from_any(f, p).wait_recv()
                if forward:
                    to_sib(f, p).start()

    pltpu.make_async_copy(w0, w0, w_sem.at[0]).wait()
    pltpu.make_async_copy(wp, wp, w_sem.at[1]).wait()
    process(tm)
    wait_frame(sib, False)
    process(sib)

    def far(d):
        base = lax.rem(y + d, ny) * CORES
        wait_frame(base + core, True)
        process(base + core)
        wait_frame(base + 1 - core, False)
        process(base + 1 - core)

    loop_peers(far)

    def lanes_of(x):
        if outs % LANES == 0:
            return x[..., pl.ds(pl.multiple_of(tm * outs, LANES), outs)]
        full = x[...].astype(jnp.float32)
        full = full.reshape(-1, channels)
        moved = pltpu.roll(full, channels - tm * outs, 1)
        return moved[:, 0:outs]

    if outs % LANES == 0:
        offset = lanes_of(bias)
    else:
        offset = lanes_of(jnp.broadcast_to(bias[...], (8, channels)))[0:1]

    def out_copy(f):
        return pltpu.make_async_remote_copy(
            src_ref=block.at[f], dst_ref=out.at[tm], send_sem=out_send.at[f],
            recv_sem=out_recv.at[tm], device_id=(f, row), device_id_type=MESH)

    def finish(f):
        conv = (prod[f, 2] + prod[jnp.maximum(f - 1, 0), 1]) + prod[jnp.maximum(f - 2, 0), 0]
        kept = lanes_of(raw.at[f, 1:1 + height]).astype(jnp.float32)
        kept = kept.reshape(height * across, outs)
        return (kept + conv + offset).astype(jnp.bfloat16)

    def give(f):
        block[f] = finish(f)
        out_copy(f).start()

    def give_far(d):
        base = lax.rem(y + d, ny) * CORES
        give(base + core)
        give(base + 1 - core)

    loop_peers(give_far)
    give(sib)
    out[tm] = finish(tm)

    def take(i, carry):
        src = lax.rem(tm + i, nt)
        pltpu.make_async_remote_copy(
            src_ref=block.at[src], dst_ref=out.at[src], send_sem=out_send.at[src],
            recv_sem=out_recv.at[src], device_id=(sib, row), device_id_type=MESH).wait()
        return carry

    lax.fori_loop(1, nt, take, 0)

    @pl.when(has_below)
    def _():
        up_copy.wait_send()

    @pl.when(has_above)
    def _():
        down_copy.wait_send()

    for p, there in ((0, has_above), (1, None), (2, has_below)):
        def drain(p=p):
            def one(d):
                to_peer(d, p).wait_send()
                to_sib(lax.rem(y + d, ny) * CORES + core, p).wait_send()
            loop_peers(one)
            to_sib(tm, p).wait_send()
        if there is None:
            drain()
        else:
            pl.when(there)(drain)


def local(nt, nr, features, gamma, beta, kernel, bias):
    _, height, across, channels = features.shape
    outs = kernel.shape[1]
    total = nt * nr
    weights = jnp.transpose(kernel, (0, 2, 3, 1, 4))
    vmem = pl.BlockSpec(memory_space=pltpu.VMEM)
    anywhere = pl.BlockSpec(memory_space=pl.ANY)
    bf16, f32 = jnp.bfloat16, jnp.float32
    dma = pltpu.SemaphoreType.DMA
    parts = pl.pallas_call(
        functools.partial(body, nt, nr),
        out_shape=jax.ShapeDtypeStruct((nt, height * across, outs), bf16),
        in_specs=[anywhere, vmem, vmem, anywhere, vmem],
        out_specs=vmem,
        scratch_shapes=[
            pltpu.VMEM((nt, height + 2, across, channels), bf16),
            pltpu.VMEM((nt, height + 2, across, 3 * channels), bf16),
            pltpu.VMEM((3, 2 * outs, 3 * channels), bf16),
            pltpu.VMEM((3, outs, 3 * channels), bf16),
            pltpu.VMEM((nt, 3, height * across, outs), f32),
            pltpu.VMEM((total, 1, LANES), f32),
            pltpu.VMEM((nt, height * across, outs), bf16),
            dma, dma((2,)), dma, dma,
            dma((2,)), dma((nt, 3)), dma((nt // CORES, 3)), dma((nt, 3)),
            dma((nt,)), dma((nt,)),
        ],
        compiler_params=pltpu.CompilerParams(collective_id=0, has_side_effects=True),
    )(features, gamma.reshape(1, -1), beta.reshape(1, -1), weights, bias.reshape(1, -1))
    return jnp.transpose(parts, (1, 0, 2)).reshape(features.shape)


def solution(mesh):
    nt, nr = mesh.shape["tm"], mesh.shape["rows"]
    in_specs = (P("tm", "rows", None, None), P(), P(), P(None, "tm", None, None, None), P())
    out_specs = P("tm", "rows", None, None)
    return jax.shard_map(functools.partial(local, nt, nr), mesh=mesh, in_specs=in_specs,
                         out_specs=out_specs, check_vma=False)
```

time: 136 us -> 25.9 us (0.19)
  the two profiles are of different devices: /device:TPU:13 before, /device:TPU:3 now
where the time goes in v1:
time: 25.9 us; the launch traced here: 25.7 us
  Pallas kernels  23.9 us (92%)
  local copies, waits for them, and re-layouts  1.84 us (7%)
    pallas_call x1, Pallas kernels, local(): pl.pallas_call(functools.partial(body, nt, nr), out_shape=jax.ShapeDtypeS...  23.9 us
    transpose x1, local copies, waits for them, and re-layouts, local(): return jnp.transpose(parts, (1, 0, 2)).reshape(features.shape)  1.08 us
    reshape x1, local copies, waits for them, and re-layouts, local(): return jnp.transpose(parts, (1, 0, 2)).reshape(features.shape)  0.76 us

profile of v1, /device:TPU:3, one launch (start us, length us, event | category | flops | bytes accessed | tf_op | source)
XLA Modules:
  0.0 25.7 jit_solution(11933308299300330104)
XLA Ops:
  0.0 23.9 %shard_map.55 = bf16[4,192,128]{2,1,0:T(8,128)(2,1)} custom-call(bf16[1,3,64,512]{3,2,1,0:T(8,128)(2,1)} %features.1, f32[1,512]{1,0:T(1,128)} %bitcast.7, f32[1,512]{1,0:T(1,128)} %bitcast.8, bf16[3,3,3,128,512]{4,3,2,1,0:T(8,128)(2,1)} %bitcast.5, f32[1,512]{1,0:T(1,128)} %bitcast.9), custom_call_target="tpu_custom_call" | custom-call | tf_op jit(solution)/shard_map/pallas_call | solution.py:320
  23.9 1.1 %copy.6 = bf16[192,4,128]{2,1,0:T(4,128)(2,1)S(1)} copy(bf16[192,4,128]{2,0,1:T(8,128)(2,1)} %bitcast.6) | data formatting | bytes 393216 | tf_op jit(solution)/shard_map/transpose | solution.py:339
  25.0 0.8 %reshape.15 = bf16[1,3,64,512]{3,2,1,0:T(8,128)(2,1)} reshape(bf16[192,4,128]{2,1,0:T(4,128)(2,1)S(1)} %copy.6) | data formatting | bytes 393216 | tf_op jit(solution)/shard_map/reshape | solution.py:339

commit v2 on v1

--- a/solution.py
+++ b/solution.py
@@ -178,42 +178,42 @@
 
     column = lax.broadcasted_iota(jnp.int32, (across, channels), 0)
 
-    def activate_row(f, i):
+    def activate_row(f, i, there=None):
         v = (raw[f, i].astype(jnp.float32) - center) * gain + shift
         v = v * 0.5
         v = v * jnp.tanh(v) + v
+        if there is not None:
+            v = jnp.where(there, v, 0.0)
         before = jnp.where(column == 0, 0.0, pltpu.roll(v, 1, 0))
         after = jnp.where(column == across - 1, 0.0, pltpu.roll(v, across - 1, 0))
         xs[f, i, :, 0:channels] = before.astype(jnp.bfloat16)
         xs[f, i, :, channels:2 * channels] = v.astype(jnp.bfloat16)
         xs[f, i, :, 2 * channels:] = after.astype(jnp.bfloat16)
 
-    def edge_row(f, i, there):
-        @pl.when(there)
-        def _():
-            activate_row(f, i)
-
-        @pl.when(jnp.logical_not(there))
-        def _():
-            xs[f, i] = jnp.zeros((across, 3 * channels), jnp.bfloat16)
-
-    def dot(f, taps, b):
-        left = xs[f, b:b + height].reshape(height * across, 3 * channels)
-        return lax.dot_general(left, taps[b], (((1,), (1,)), ((), ())),
-                               preferred_element_type=jnp.float32)
-
-    def process(f):
+    def activate(f):
+        activate_row(f, 0, has_above)
         for i in range(1, height + 1):
             activate_row(f, i)
-        edge_row(f, 0, has_above)
-        edge_row(f, height + 1, has_below)
-        pair = dot(f, wp, 0) + dot(f, wp, 1) + dot(f, wp, 2)
-        prod[f, 1] = pair[:, 0:outs]
-        prod[f, 2] = pair[:, outs:2 * outs]
-
-        @pl.when(jnp.logical_or(f == 0, f + 2 < nt))
+        activate_row(f, height + 1, has_below)
+
+    def dot(base, taps):
+        total_out = None
+        for b in range(3):
+            left = xs[pl.ds(base, CORES), b:b + height]
+            left = left.reshape(CORES * height * across, 3 * channels)
+            part = lax.dot_general(left, taps[b], (((1,), (1,)), ((), ())),
+                                   preferred_element_type=jnp.float32)
+            total_out = part if total_out is None else total_out + part
+        return total_out.reshape(CORES, height, across, -1)
+
+    def convolve(base):
+        pair = dot(base, wp)
+        prod[1, pl.ds(base, CORES)] = pair[..., 0:outs]
+        prod[2, pl.ds(base, CORES)] = pair[..., outs:2 * outs]
+
+        @pl.when(jnp.logical_or(base == 0, base + 2 < nt))
         def _():
-            prod[f, 0] = dot(f, w0, 0) + dot(f, w0, 1) + dot(f, w0, 2)
+            prod[0, pl.ds(base, CORES)] = dot(base, w0)
 
     def wait_frame(f, forward):
         from_any(f, 1).wait_recv()
@@ -228,41 +228,49 @@
 
     pltpu.make_async_copy(w0, w0, w_sem.at[0]).wait()
     pltpu.make_async_copy(wp, wp, w_sem.at[1]).wait()
-    process(tm)
+    activate(tm)
     wait_frame(sib, False)
-    process(sib)
+    activate(sib)
+    convolve(y * CORES)
 
     def far(d):
         base = lax.rem(y + d, ny) * CORES
         wait_frame(base + core, True)
-        process(base + core)
+        activate(base + core)
         wait_frame(base + 1 - core, False)
-        process(base + 1 - core)
+        activate(base + 1 - core)
+        convolve(base)
 
     loop_peers(far)
 
+    direct = outs % LANES == 0
+
     def lanes_of(x):
-        if outs % LANES == 0:
+        if direct:
             return x[..., pl.ds(pl.multiple_of(tm * outs, LANES), outs)]
         full = x[...].astype(jnp.float32)
-        full = full.reshape(-1, channels)
-        moved = pltpu.roll(full, channels - tm * outs, 1)
-        return moved[:, 0:outs]
-
-    if outs % LANES == 0:
+        lead = full.shape[:-1]
+        moved = pltpu.roll(full.reshape(-1, channels), channels - tm * outs, 1)
+        return moved[:, 0:outs].reshape(*lead, outs)
+
+    if direct:
         offset = lanes_of(bias)
     else:
         offset = lanes_of(jnp.broadcast_to(bias[...], (8, channels)))[0:1]
 
+    def landing(src):
+        if direct:
+            return out.at[0, :, :, pl.ds(pl.multiple_of(src * outs, LANES), outs)]
+        return out.at[src]
+
     def out_copy(f):
         return pltpu.make_async_remote_copy(
-            src_ref=block.at[f], dst_ref=out.at[tm], send_sem=out_send.at[f],
+            src_ref=block.at[f], dst_ref=landing(tm), send_sem=out_send.at[f],
             recv_sem=out_recv.at[tm], device_id=(f, row), device_id_type=MESH)
 
     def finish(f):
-        conv = (prod[f, 2] + prod[jnp.maximum(f - 1, 0), 1]) + prod[jnp.maximum(f - 2, 0), 0]
+        conv = (prod[2, f] + prod[1, jnp.maximum(f - 1, 0)]) + prod[0, jnp.maximum(f - 2, 0)]
         kept = lanes_of(raw.at[f, 1:1 + height]).astype(jnp.float32)
-        kept = kept.reshape(height * across, outs)
         return (kept + conv + offset).astype(jnp.bfloat16)
 
     def give(f):
@@ -276,12 +284,15 @@
 
     loop_peers(give_far)
     give(sib)
-    out[tm] = finish(tm)
+    if direct:
+        out[0, :, :, pl.ds(pl.multiple_of(tm * outs, LANES), outs)] = finish(tm)
+    else:
+        out[tm] = finish(tm)
 
     def take(i, carry):
         src = lax.rem(tm + i, nt)
         pltpu.make_async_remote_copy(
-            src_ref=block.at[src], dst_ref=out.at[src], send_sem=out_send.at[src],
+            src_ref=block.at[src], dst_ref=landing(src), send_sem=out_send.at[src],
             recv_sem=out_recv.at[src], device_id=(sib, row), device_id_type=MESH).wait()
         return carry
 
@@ -313,13 +324,15 @@
     outs = kernel.shape[1]
     total = nt * nr
     weights = jnp.transpose(kernel, (0, 2, 3, 1, 4))
+    direct = outs % LANES == 0
+    shape = features.shape if direct else (nt, height, across, outs)
     vmem = pl.BlockSpec(memory_space=pltpu.VMEM)
     anywhere = pl.BlockSpec(memory_space=pl.ANY)
     bf16, f32 = jnp.bfloat16, jnp.float32
     dma = pltpu.SemaphoreType.DMA
     parts = pl.pallas_call(
         functools.partial(body, nt, nr),
-        out_shape=jax.ShapeDtypeStruct((nt, height * across, outs), bf16),
+        out_shape=jax.ShapeDtypeStruct(shape, bf16),
         in_specs=[anywhere, vmem, vmem, anywhere, vmem],
         out_specs=vmem,
         scratch_shapes=[
@@ -327,16 +340,18 @@
             pltpu.VMEM((nt, height + 2, across, 3 * channels), bf16),
             pltpu.VMEM((3, 2 * outs, 3 * channels), bf16),
             pltpu.VMEM((3, outs, 3 * channels), bf16),
-            pltpu.VMEM((nt, 3, height * across, outs), f32),
+            pltpu.VMEM((3, nt, height, across, outs), f32),
             pltpu.VMEM((total, 1, LANES), f32),
-            pltpu.VMEM((nt, height * across, outs), bf16),
+            pltpu.VMEM((nt, height, across, outs), bf16),
             dma, dma((2,)), dma, dma,
             dma((2,)), dma((nt, 3)), dma((nt // CORES, 3)), dma((nt, 3)),
             dma((nt,)), dma((nt,)),
         ],
         compiler_params=pltpu.CompilerParams(collective_id=0, has_side_effects=True),
     )(features, gamma.reshape(1, -1), beta.reshape(1, -1), weights, bias.reshape(1, -1))
-    return jnp.transpose(parts, (1, 0, 2)).reshape(features.shape)
+    if direct:
+        return parts
+    return jnp.transpose(parts, (1, 2, 0, 3)).reshape(features.shape)
 
 
 def solution(mesh):

time: 25.9 us -> 26 us (level)
    unnamed x0 -> x1, local copies, waits for them, and re-layouts: none -> 1.62 us
    transpose x1 -> x0, local copies, waits for them, and re-layouts: 1.08 us -> none  [local(): return jnp.transpose(parts, (1, 0, 2)).reshape(features.shape)]
    reshape x1 -> x0, local copies, waits for them, and re-layouts: 0.76 us -> none  [local(): return jnp.transpose(parts, (1, 0, 2)).reshape(features.shape)]
where the time goes in v2:
time: 26 us; the launch traced here: 25.6 us
  Pallas kernels  24 us (92%)
  local copies, waits for them, and re-layouts  1.62 us (6%)
    pallas_call x1, Pallas kernels, local(): pl.pallas_call(functools.partial(body, nt, nr), out_shape=jax.ShapeDtypeS...  24 us
    unnamed x1, local copies, waits for them, and re-layouts  1.62 us

profile of v2, /device:TPU:3, one launch (start us, length us, event | category | flops | bytes accessed | tf_op | source)
XLA Modules:
  0.0 25.6 jit_solution(3582926894451985573)
XLA Ops:
  0.0 24.0 %shard_map.55 = bf16[1,3,64,512]{3,2,1,0:T(8,128)(2,1)} custom-call(bf16[1,3,64,512]{3,2,1,0:T(8,128)(2,1)} %features.1, f32[1,512]{1,0:T(1,128)} %bitcast.5, f32[1,512]{1,0:T(1,128)} %bitcast.6, bf16[3,3,3,128,512]{4,3,2,1,0:T(8,128)(2,1)} %bitcast.4, f32[1,512]{1,0:T(1,128)} %bitcast.7), custom_call_target="tpu_custom_call" | custom-call | tf_op jit(solution)/shard_map/pallas_call | solution.py:333
  24.0 1.6 %copy.7 = bf16[1,3,64,512]{3,2,1,0:T(8,128)(2,1)} copy(bf16[1,3,64,512]{3,2,1,0:T(8,128)(2,1)} %shard_map.55) | data formatting | bytes 393216

commit v3 on v2

--- a/solution.py
+++ b/solution.py
@@ -12,6 +12,7 @@
 LANES = 128
 MESH = pl.DeviceIdType.MESH
 CORES = 2
+VMEM_LIMIT = 67043328 - 262144
 
 
 def group_sum(x, span):
@@ -284,10 +285,9 @@
 
     loop_peers(give_far)
     give(sib)
-    if direct:
-        out[0, :, :, pl.ds(pl.multiple_of(tm * outs, LANES), outs)] = finish(tm)
-    else:
-        out[tm] = finish(tm)
+    block[tm] = finish(tm)
+    keep = pltpu.make_async_copy(block.at[tm], landing(tm), feat_sem)
+    keep.start()
 
     def take(i, carry):
         src = lax.rem(tm + i, nt)
@@ -297,6 +297,7 @@
         return carry
 
     lax.fori_loop(1, nt, take, 0)
+    keep.wait()
 
     @pl.when(has_below)
     def _():
@@ -327,14 +328,14 @@
     direct = outs % LANES == 0
     shape = features.shape if direct else (nt, height, across, outs)
     vmem = pl.BlockSpec(memory_space=pltpu.VMEM)
-    anywhere = pl.BlockSpec(memory_space=pl.ANY)
+    hbm = pl.BlockSpec(memory_space=pltpu.HBM)
     bf16, f32 = jnp.bfloat16, jnp.float32
     dma = pltpu.SemaphoreType.DMA
     parts = pl.pallas_call(
         functools.partial(body, nt, nr),
         out_shape=jax.ShapeDtypeStruct(shape, bf16),
-        in_specs=[anywhere, vmem, vmem, anywhere, vmem],
-        out_specs=vmem,
+        in_specs=[hbm, vmem, vmem, hbm, vmem],
+        out_specs=pl.BlockSpec(memory_space=pl.ANY),
         scratch_shapes=[
             pltpu.VMEM((nt, height + 2, across, channels), bf16),
             pltpu.VMEM((nt, height + 2, across, 3 * channels), bf16),
@@ -347,7 +348,8 @@
             dma((2,)), dma((nt, 3)), dma((nt // CORES, 3)), dma((nt, 3)),
             dma((nt,)), dma((nt,)),
         ],
-        compiler_params=pltpu.CompilerParams(collective_id=0, has_side_effects=True),
+        compiler_params=pltpu.CompilerParams(collective_id=0, has_side_effects=True,
+                                             vmem_limit_bytes=VMEM_LIMIT),
     )(features, gamma.reshape(1, -1), beta.reshape(1, -1), weights, bias.reshape(1, -1))
     if direct:
         return parts

time: 26 us -> 25.4 us (0.977)
  Pallas kernels: 24 us -> 23.4 us
    pallas_call x1, Pallas kernels: 24 us -> 23.4 us  [local(): pl.pallas_call(functools.partial(body, nt, nr), out_shape=jax.ShapeDtypeS...]
where the time goes in v3:
time: 25.4 us; the launch traced here: 25 us
  Pallas kernels  23.4 us (92%)
  local copies, waits for them, and re-layouts  1.62 us (6%)
    pallas_call x1, Pallas kernels, local(): pl.pallas_call(functools.partial(body, nt, nr), out_shape=jax.ShapeDtypeS...  23.4 us
    unnamed x1, local copies, waits for them, and re-layouts  1.62 us

profile of v3, /device:TPU:3, one launch (start us, length us, event | category | flops | bytes accessed | tf_op | source)
XLA Modules:
  0.0 25.0 jit_solution(9648823242765353699)
XLA Ops:
  0.0 23.4 %shard_map.55 = bf16[1,3,64,512]{3,2,1,0:T(8,128)(2,1)} custom-call(bf16[1,3,64,512]{3,2,1,0:T(8,128)(2,1)} %features.1, f32[1,512]{1,0:T(1,128)} %bitcast.5, f32[1,512]{1,0:T(1,128)} %bitcast.6, bf16[3,3,3,128,512]{4,3,2,1,0:T(8,128)(2,1)} %bitcast.4, f32[1,512]{1,0:T(1,128)} %bitcast.7), custom_call_target="tpu_custom_call" | custom-call | tf_op jit(solution)/shard_map/pallas_call | solution.py:334
  23.4 1.6 %copy.7 = bf16[1,3,64,512]{3,2,1,0:T(8,128)(2,1)} copy(bf16[1,3,64,512]{3,2,1,0:T(8,128)(2,1)} %shard_map.55) | data formatting | bytes 393216
